TPU v7x, 32 devices: a whole 2x2x4 slice. The times are simulated.
32 devices in a mesh: blk: 8 (over z, y), grp: 4 (over x, core).
Axes of the slice: x: 2, y: 2, z: 4, core: 2. Of those that a mesh axis runs over, the one named last changes fastest.
Arguments:
- frames: bfloat16 [4, 2048, 1024], P('grp', 'blk'), may hold values from -16 to 16
- utt_lengths: int32 [4], replicated, may hold values from 1 to 4096, 8192 in all
- attn_gain: float32 [1024], replicated, may hold values from 0.25 to 1.75
- w_qkv: bfloat16 [1024, 3072], P(None, 'grp'), may hold values from -4 to 4
- w_out: bfloat16 [1024, 1024], replicated, may hold values from -0.375 to 0.375
- conv_gain: float32 [1024], replicated, may hold values from 0.25 to 1.75
- w_glu: bfloat16 [1024, 2048], replicated, may hold values from -0.1875 to 0.1875
- w_depth: float32 [31, 1024], replicated, may hold values from -1 to 1
- depth_gain: float32 [1024], replicated, may hold values from 0.25 to 1.75
- w_proj: bfloat16 [1024, 1024], replicated, may hold values from -0.1875 to 0.1875
Outputs:
- block_out: bfloat16 [4, 2048, 1024], P('grp', 'blk')
Inputs may be any that keep to these rules, and one draw needn't show every extreme that they name: `utt_lengths`: they sum to 8192 and the longest is exactly 4096.
All inputs are finite; a program needn't handle non-finite values.
Results may differ from a plain program's by a relative error of at most 0.0095.
Values may be sent and summed in bfloat16 or wider, within the bound.
A program may use at most 192 MiB of HBM per device.

v0:
```python
import functools
import math

import jax
import jax.numpy as jnp
from jax import lax
from jax.experimental import pallas as pl
from jax.experimental.pallas import tpu as pltpu
from jax.sharding import PartitionSpec as P

HEADS = 16

epsilon = 1e-05
big_negative = -1e30
MESH = pl.DeviceIdType.MESH
VMEM_LIMIT = 56 * 1024 * 1024


def normalize(values, row_gain):
    center = values - jnp.mean(values, axis=-1, keepdims=True)
    spread = jnp.mean(center * center, axis=-1, keepdims=True)
    return center * lax.rsqrt(spread + epsilon) * row_gain


def starts_of(lengths_ref):
    starts, total = [], jnp.int32(0)
    for c in range(lengths_ref.shape[0]):
        starts.append(total)
        total = total + lengths_ref[c]
    return starts


def seg_at(starts, positions):
    seg = jnp.full(positions.shape, -1, jnp.int32)
    for start in starts:
        seg = seg + jnp.where(positions >= start, 1, 0)
    return seg


def remote(src, dst, send, recv, blk, grp):
    return pltpu.make_async_remote_copy(
        src_ref=src, dst_ref=dst, send_sem=send, recv_sem=recv,
        device_id=(blk, grp), device_id_type=MESH,
    )


def place_of(window, groups):
    return (window % 2) * (groups // 2) + window // 2


def window_at(place, groups):
    return (place % (groups // 2)) * 2 + place // (groups // 2)


def project_kernel(
    blocks, groups, chunks, head_width, lengths_ref, frames_ref, gain_ref, w_ref,
    q_ref, k_ref, v_ref,
    norm, held, weights, w_sem, d_sem, x_sem, y_sem, p_sem, r_sem,
):
    b, g = lax.axis_index("blk"), lax.axis_index("grp")
    np_ = blocks // groups
    pairs = groups // 2
    rows, width = norm.shape[1:]
    columns = weights.shape[1]
    heads = columns // (3 * head_width)
    place, share, core, chip = b // np_, b % np_, g % 2, g // 2
    mine = window_at(place, groups)
    source_chip = mine // 2
    partner = g + 1 - 2 * core
    if np_ == 1:
        w_src = w_ref
    else:
        w_src = w_ref.at[:, pl.ds(pl.multiple_of(share * columns, 128), columns)]
    w_copy = pltpu.make_async_copy(w_src, weights, w_sem)
    w_copy.start()
    target = place_of(g, groups) * np_ + share
    target_core = place % 2
    self_kept = jnp.logical_and(target == b, target_core == core)

    def direct(c):
        u = b * chunks + c
        return remote(
            norm.at[c], held.at[u], d_sem.at[c], r_sem.at[u], target, 2 * chip + target_core
        )

    for c in range(chunks):
        part = frames_ref[c * rows:(c + 1) * rows, :].astype(jnp.float32)
        norm[c] = normalize(part, gain_ref[...]).astype(jnp.bfloat16)

        @pl.when(jnp.logical_not(self_kept))
        def _():
            direct(c).start()

        @pl.when(self_kept)
        def _():
            held[b * chunks + c] = norm[c]

    lane = lax.broadcasted_iota(jnp.int32, (rows, 128), 1)
    row = lax.broadcasted_iota(jnp.int32, (rows, 128), 0)
    scale = head_width ** (-0.5) * math.log2(math.e)
    starts = starts_of(lengths_ref)

    def padded(part):
        return jnp.concatenate([part, jnp.zeros((rows, 128 - head_width), jnp.float32)], axis=1)

    def project(u):
        out = jnp.dot(held[u], weights[...], preferred_element_type=jnp.float32)
        seg = seg_at(starts, mine * blocks * chunks * rows + u * rows + row)
        same = lane - head_width == seg
        at = pl.ds(pl.multiple_of(u * rows, rows), rows)
        for h in range(heads):
            o = 3 * head_width * h
            q = padded(out[:, o:o + head_width] * scale)
            k = padded(out[:, o + head_width:o + 2 * head_width])
            v = padded(out[:, o + 2 * head_width:o + 3 * head_width])
            q = jnp.where(lane < head_width, q, jnp.where(same, big_negative, 0.0))
            k = jnp.where(lane < head_width, k, jnp.where(same, 0.0, 1.0))
            v = jnp.where(lane < head_width, v, jnp.where(lane == head_width, 1.0, 0.0))
            q_ref[h, at, :] = q.astype(jnp.bfloat16)
            k_ref[h, at, :] = k.astype(jnp.bfloat16)
            v_ref[h, at, :] = v.astype(jnp.bfloat16)

    def pair(u):
        return remote(held.at[u], held.at[u], p_sem.at[u], r_sem.at[u], b, partner)

    def across(u, i):
        other = b - share + (share + i) % np_
        return remote(held.at[u], held.at[u], y_sem.at[u, i], r_sem.at[u], other, g)

    def over(u, k):
        return remote(held.at[u], held.at[u], x_sem.at[u, k], r_sem.at[u], b, 2 * k + core)

    def unit(j, i):
        n = j // chunks
        n = n + place // pairs * (pairs - 1 - 2 * n)
        return ((2 * n + core) * np_ + (share + i) % np_) * chunks + j % chunks

    count = pairs * chunks

    def take(j, carry):
        u = unit(j, 0)

        @pl.when(jnp.logical_not(jnp.logical_and(u // chunks == b, mine == g)))
        def _():
            pair(u).wait_recv()

        for k in range(pairs):
            @pl.when(jnp.logical_and(chip == source_chip, chip != k))
            def _():
                over(u, k).start()

        for i in range(1, np_):
            across(u, i).start()
        pair(u).start()
        return carry

    lax.fori_loop(0, count, take, 0)
    w_copy.wait()

    def own(j, carry):
        project(unit(j, 0))
        return carry

    lax.fori_loop(0, count, own, 0)

    def pass_on(j, carry):
        for i in range(1, np_):
            u = unit(j, i)
            pair(u).wait_recv()
            pair(u).start()
            project(u)
        return carry

    if np_ > 1:
        lax.fori_loop(0, count, pass_on, 0)

    def rest(j, carry):
        n = j // (np_ * chunks)
        n = n + place // pairs * (pairs - 1 - 2 * n)
        i = j // chunks % np_
        u = ((2 * n + 1 - core) * np_ + (share + i) % np_) * chunks + j % chunks
        pair(u).wait_recv()
        project(u)
        return carry

    lax.fori_loop(0, count * np_, rest, 0)

    for c in range(chunks):
        @pl.when(jnp.logical_not(self_kept))
        def _():
            direct(c).wait_send()

    def drain(j, carry):
        u = unit(j, 0)
        for k in range(pairs):
            @pl.when(jnp.logical_and(chip == source_chip, chip != k))
            def _():
                over(u, k).wait_send()

        for i in range(1, np_):
            across(u, i).wait_send()
        for i in range(np_):
            pair(unit(j, i)).wait_send()
        return carry

    lax.fori_loop(0, count, drain, 0)


def attend(head_width, q_ref, k_ref, v_ref, at):
    outs = []
    for h in range(q_ref.shape[0]):
        scores = lax.dot_general(
            q_ref[h, at, :], k_ref[h], (((1,), (1,)), ((), ())),
            preferred_element_type=jnp.float32,
        )
        top = jnp.max(scores, axis=1, keepdims=True)
        weights = jnp.exp2(scores - top).astype(jnp.bfloat16)
        mixed = jnp.dot(weights, v_ref[h], preferred_element_type=jnp.float32)
        outs.append(mixed[:, :head_width] / mixed[:, head_width:head_width + 1])
    return jnp.concatenate(outs, axis=1).astype(jnp.bfloat16)


def projected(frames, lengths, attn_gain, w_qkv, blocks, groups, head_width):
    rows, width = frames.shape
    np_ = blocks // groups
    columns = w_qkv.shape[1] // np_
    heads = columns // (3 * head_width)
    window = rows * blocks
    chunks = 2 if rows % 32 == 0 else 1
    vm = pl.BlockSpec(memory_space=pltpu.VMEM)
    wide = jax.ShapeDtypeStruct((heads, window, 128), jnp.bfloat16)
    return pl.pallas_call(
        functools.partial(project_kernel, blocks, groups, chunks, head_width),
        out_shape=[wide] * 3,
        in_specs=[pl.BlockSpec(memory_space=pltpu.SMEM), vm, vm, pl.BlockSpec(memory_space=pl.ANY)],
        out_specs=[vm] * 3,
        scratch_shapes=[
            pltpu.VMEM((chunks, rows // chunks, width), jnp.bfloat16),
            pltpu.VMEM((blocks * chunks, rows // chunks, width), jnp.bfloat16),
            pltpu.VMEM((width, columns), jnp.bfloat16),
            pltpu.SemaphoreType.DMA(()),
            pltpu.SemaphoreType.DMA((chunks,)),
            pltpu.SemaphoreType.DMA((blocks * chunks, groups // 2)),
            pltpu.SemaphoreType.DMA((blocks * chunks, np_)),
            pltpu.SemaphoreType.DMA((blocks * chunks,)),
            pltpu.SemaphoreType.DMA((blocks * chunks,)),
        ],
        compiler_params=pltpu.CompilerParams(has_side_effects=True, vmem_limit_bytes=VMEM_LIMIT),
        name="project",
    )(lengths, frames, attn_gain[None], w_qkv)


def finish_kernel(
    blocks, groups, head_width, lengths_ref, q_ref, k_ref, v_ref, frames_ref, conv_gain_ref, depth_ref, depth_gain_ref,
    w_out_ref, w_glu_ref, w_proj_ref,
    out_ref,
    mixed_heads, parts, w_out, w_glu, w_proj, masks, residual, edge, halo, extended, mixed,
    s_sem, r_sem, w_sem, hs_sem, hr_sem,
):
    b, g = lax.axis_index("blk"), lax.axis_index("grp")
    np_ = blocks // groups
    rows, width = frames_ref.shape
    taps = depth_ref.shape[0]
    half = (taps - 1) // 2
    rim = halo.shape[1]
    mine, unit = window_at(b // np_, groups), g * np_ + b % np_
    home = mine == g
    position = g * blocks + b
    after = (position + 1) % (blocks * groups)
    before = (position + blocks * groups - 1) % (blocks * groups)

    def send(s):
        return remote(
            mixed_heads.at[s], parts.at[unit], s_sem.at[s], r_sem.at[unit], s, mine
        )

    loads = [
        pltpu.make_async_copy(w_out_ref, w_out, w_sem.at[0]),
        pltpu.make_async_copy(w_glu_ref, w_glu, w_sem.at[1]),
        pltpu.make_async_copy(w_proj_ref, w_proj, w_sem.at[2]),
    ]
    for load in loads:
        load.start()

    def attend_for(i, carry):
        s = (b + 1 + i) % blocks
        at = pl.ds(pl.multiple_of(s * rows, rows), rows)
        mixed_heads[s] = attend(head_width, q_ref, k_ref, v_ref, at)
        kept = jnp.logical_and(home, s == b)

        @pl.when(jnp.logical_not(kept))
        def _():
            send(s).start()

        @pl.when(kept)
        def _():
            parts[unit] = mixed_heads[s]

        return carry

    lax.fori_loop(0, blocks, attend_for, 0)

    row = position * rows + lax.broadcasted_iota(jnp.int32, (rows, 128), 0)
    low = jnp.zeros((rows, 128), jnp.int32)
    high = jnp.full((rows, 128), blocks * groups * rows, jnp.int32)
    for start in starts_of(lengths_ref):
        low = jnp.where(row >= start, jnp.maximum(low, start), low)
        high = jnp.where(row < start, jnp.minimum(high, start), high)
    for t in range(taps):
        at = row + (t - half)
        masks[t] = jnp.where(jnp.logical_and(at >= low, at < high), 1.0, 0.0)

    for i in range(blocks):
        @pl.when(jnp.logical_not(jnp.logical_and(home, unit == i)))
        def _():
            remote(parts.at[i], parts.at[i], s_sem.at[i], r_sem.at[i], b, g).wait_recv()

    attended = jnp.concatenate([parts[i] for i in range(blocks)], axis=1)
    loads[0].wait()
    total = frames_ref[...].astype(jnp.float32) + jnp.dot(
        attended, w_out[...], preferred_element_type=jnp.float32
    )
    residual[...] = total.astype(jnp.bfloat16)
    conv_in = normalize(residual[...].astype(jnp.float32), conv_gain_ref[...]).astype(jnp.bfloat16)
    loads[1].wait()
    step = 256
    for n in range(0, width, step):
        a = jnp.dot(conv_in, w_glu[:, n:n + step], preferred_element_type=jnp.float32)
        gate = jnp.dot(
            conv_in, w_glu[:, width + n:width + n + step], preferred_element_type=jnp.float32
        )
        gated = (a * jax.nn.sigmoid(gate)).astype(jnp.bfloat16)
        edge[0, :, n:n + step] = gated[:rim]
        edge[1, :, n:n + step] = gated[rows - rim:]
        extended[rim:rim + rows, n:n + step] = gated.astype(jnp.float32)

    to_next = remote(
        edge.at[1], halo.at[0], hs_sem.at[1], hr_sem.at[0], after % blocks, after // blocks
    )
    to_prev = remote(
        edge.at[0], halo.at[1], hs_sem.at[0], hr_sem.at[1], before % blocks, before // blocks
    )
    to_next.start()
    to_prev.start()

    strip = min(64, rows)

    def convolve(strips):
        def column(c, carry):
            cols = pl.ds(pl.multiple_of(c * 128, 128), 128)
            for r in strips:
                acc = jnp.zeros((strip, 128), jnp.float32)
                for t in range(taps):
                    e = rim + r + t - half
                    x = extended[e:e + strip, cols] * masks[t, r:r + strip, :]
                    acc = acc + x * depth_ref[t:t + 1, cols]
                mixed[r:r + strip, cols] = acc
            return carry

        lax.fori_loop(0, width // 128, column, 0)

    every = list(range(0, rows, strip))
    convolve(every[1:-1])
    to_next.wait_recv()
    to_prev.wait_recv()
    extended[:rim, :] = halo[0].astype(jnp.float32)
    extended[rim + rows:, :] = halo[1].astype(jnp.float32)
    convolve([every[0], every[-1]])
    normed = normalize(mixed[...], depth_gain_ref[...])
    activated = (normed * jax.nn.sigmoid(normed)).astype(jnp.bfloat16)
    loads[2].wait()
    out_ref[0] = (
        residual[...].astype(jnp.float32)
        + jnp.dot(activated, w_proj[...], preferred_element_type=jnp.float32)
    ).astype(out_ref.dtype)

    for i in range(blocks):
        @pl.when(jnp.logical_not(jnp.logical_and(home, b == i)))
        def _():
            send(i).wait_send()

    to_next.wait_send()
    to_prev.wait_send()


def body(
    frames, utt_lengths, attn_gain, w_qkv, w_out, conv_gain, w_glu, w_depth, depth_gain, w_proj
):
    rows, width = frames.shape[1:]
    blocks, groups = lax.axis_size("blk"), lax.axis_size("grp")
    head_width = width // HEADS
    q, k, v = projected(frames[0], utt_lengths, attn_gain, w_qkv, blocks, groups, head_width)
    taps = w_depth.shape[0]
    rim = -(-(taps // 2) // 16) * 16
    vm = pl.BlockSpec(memory_space=pltpu.VMEM)
    hbm = pl.BlockSpec(memory_space=pl.ANY)
    return pl.pallas_call(
        functools.partial(finish_kernel, blocks, groups, head_width),
        out_shape=jax.ShapeDtypeStruct((1, rows, width), jnp.bfloat16),
        in_specs=[pl.BlockSpec(memory_space=pltpu.SMEM)] + [vm] * 7 + [hbm] * 3,
        out_specs=vm,
        scratch_shapes=[
            pltpu.VMEM((blocks, rows, q.shape[0] * head_width), jnp.bfloat16),
            pltpu.VMEM((blocks, rows, q.shape[0] * head_width), jnp.bfloat16),
            pltpu.VMEM(w_out.shape, jnp.bfloat16),
            pltpu.VMEM(w_glu.shape, jnp.bfloat16),
            pltpu.VMEM(w_proj.shape, jnp.bfloat16),
            pltpu.VMEM((taps, rows, 128), jnp.float32),
            pltpu.VMEM((rows, width), jnp.bfloat16),
            pltpu.VMEM((2, rim, width), jnp.bfloat16),
            pltpu.VMEM((2, rim, width), jnp.bfloat16),
            pltpu.VMEM((rows + 2 * rim, width), jnp.float32),
            pltpu.VMEM((rows, width), jnp.float32),
            pltpu.SemaphoreType.DMA((blocks,)),
            pltpu.SemaphoreType.DMA((blocks,)),
            pltpu.SemaphoreType.DMA((3,)),
            pltpu.SemaphoreType.DMA((2,)),
            pltpu.SemaphoreType.DMA((2,)),
        ],
        compiler_params=pltpu.CompilerParams(has_side_effects=True, vmem_limit_bytes=VMEM_LIMIT),
        name="finish",
    )(
        utt_lengths, q, k, v, frames[0], conv_gain[None], w_depth, depth_gain[None],
        w_out, w_glu, w_proj,
    )


def solution(mesh):
    in_specs = (P("grp", "blk", None), P(), P(), P(None, "grp"), P(), P(), P(), P(), P(), P())
    out_specs = P("grp", "blk", None)
    return jax.shard_map(body, mesh=mesh, in_specs=in_specs, out_specs=out_specs, check_vma=False)
```

profile of v0, /device:TPU:0, one launch (start us, length us, event | category | flops | bytes accessed | tf_op | source)
XLA Modules:
  0.0 91.7 jit_solution(2021168914797537337)
XLA Ops:
  0.0 44.1 %project.1 = (bf16[2,2048,128]{2,1,0:T(8,128)(2,1)}, bf16[2,2048,128]{2,1,0:T(8,128)(2,1)}, bf16[2,2048,128]{2,1,0:T(8,128)(2,1)}) custom-call(s32[4]{0:T(128)} %lengths_ref.3, bf16[256,1024]{1,0:T(8,128)(2,1)} %bitcast.4, f32[1,1024]{1,0:T(1,128)} %bitcast.6, bf16[1024,768]{1,0:T(8,128)(2,1)} %w_ref.1), custom_call_target="tpu_custom_call" | custom-call | tf_op jit(solution)/shard_map/project/pallas_call | solution.py:232
  44.1 45.8 %finish.1 = bf16[1,256,1024]{2,1,0:T(8,128)(2,1)} custom-call(s32[4]{0:T(128)} %lengths_ref.3, bf16[2,2048,128]{2,1,0:T(8,128)(2,1)} %get-tuple-element.8.q_ref, bf16[2,2048,128]{2,1,0:T(8,128)(2,1)} %get-tuple-element.9.k_ref, bf16[2,2048,128]{2,1,0:T(8,128)(2,1)} %get-tuple-element.10.v_ref, bf16[256,1024]{1,0:T(8,128)(2,1)} %bitcast.5, ...), custom_call_target="tpu_custom_call" | custom-call | tf_op jit(solution)/shard_map/finish/pallas_call | solution.py:397
  89.9 1.9 %copy.12 = bf16[1,256,1024]{2,1,0:T(8,128)(2,1)} copy(bf16[1,256,1024]{2,1,0:T(8,128)(2,1)} %finish.1) | data formatting | bytes 1048576
where the time goes:
time: 91.9 us; the launch traced here: 91.7 us
  Pallas kernels  89.9 us (98%)
  local copies, waits for them, and re-layouts  1.87 us (2%)
    pallas_call x1, Pallas kernels, body(): pl.pallas_call(functools.partial(finish_kernel, blocks, groups, head_widt...  45.8 us
    pallas_call x1, Pallas kernels, projected(): pl.pallas_call(functools.partial(project_kernel, blocks, groups, chunks,...  44.1 us
    unnamed x1, local copies, waits for them, and re-layouts  1.87 us

commit v1 on v0

v1 whole, which is shorter than its diff:
```python
import functools
import math

import jax
import jax.numpy as jnp
from jax import lax
from jax.experimental import pallas as pl
from jax.experimental.pallas import tpu as pltpu
from jax.sharding import PartitionSpec as P

HEADS = 16

epsilon = 1e-05
big_negative = -1e30
MESH = pl.DeviceIdType.MESH
VMEM_LIMIT = 56 * 1024 * 1024


def normalize(values, row_gain):
    center = values - jnp.mean(values, axis=-1, keepdims=True)
    spread = jnp.mean(center * center, axis=-1, keepdims=True)
    return center * lax.rsqrt(spread + epsilon) * row_gain


def starts_of(lengths_ref):
    starts, total = [], jnp.int32(0)
    for c in range(lengths_ref.shape[0]):
        starts.append(total)
        total = total + lengths_ref[c]
    return starts


def seg_at(starts, positions):
    seg = jnp.full(positions.shape, -1, jnp.int32)
    for start in starts:
        seg = seg + jnp.where(positions >= start, 1, 0)
    return seg


def remote(src, dst, send, recv, blk, grp):
    return pltpu.make_async_remote_copy(
        src_ref=src, dst_ref=dst, send_sem=send, recv_sem=recv,
        device_id=(blk, grp), device_id_type=MESH,
    )


def place_of(window, groups):
    return (window % 2) * (groups // 2) + window // 2


def window_at(place, groups):
    return (place % (groups // 2)) * 2 + place // (groups // 2)


def block_kernel(
    blocks, groups, chunks, head_width,
    lengths_ref, frames_ref, gain_ref, conv_gain_ref, depth_ref, depth_gain_ref,
    w_ref, w_out_ref, w_glu_ref, w_proj_ref,
    out_ref,
    norm, held, weights, q_ref, k_ref, v_ref,
    mixed_heads, parts, w_out, w_glu, w_proj, masks, residual, edge, halo, extended, mixed,
    load_sem, d_sem, x_sem, y_sem, p_sem, r_sem, s_sem, a_sem, hs_sem, hr_sem,
):
    b, g = lax.axis_index("blk"), lax.axis_index("grp")
    np_ = blocks // groups
    pairs = groups // 2
    rows, width = norm.shape[1:]
    block = rows * chunks
    columns = weights.shape[1]
    heads = columns // (3 * head_width)
    taps = depth_ref.shape[0]
    half = (taps - 1) // 2
    rim = halo.shape[1]
    place, share, core, chip = b // np_, b % np_, g % 2, g // 2
    mine = window_at(place, groups)
    source_chip = mine // 2
    partner = g + 1 - 2 * core
    unit_index = g * np_ + share
    home = mine == g
    position = g * blocks + b
    if np_ == 1:
        w_src = w_ref
    else:
        w_src = w_ref.at[:, pl.ds(pl.multiple_of(share * columns, 128), columns)]
    loads = [
        pltpu.make_async_copy(w_src, weights, load_sem.at[0]),
        pltpu.make_async_copy(w_out_ref, w_out, load_sem.at[1]),
        pltpu.make_async_copy(w_glu_ref, w_glu, load_sem.at[2]),
        pltpu.make_async_copy(w_proj_ref, w_proj, load_sem.at[3]),
    ]
    loads[0].start()
    target = place_of(g, groups) * np_ + share
    target_core = place % 2
    self_kept = jnp.logical_and(target == b, target_core == core)

    def direct(c):
        u = b * chunks + c
        return remote(
            norm.at[c], held.at[u], d_sem.at[c], r_sem.at[u], target, 2 * chip + target_core
        )

    with jax.named_scope("norm"):
        for c in range(chunks):
            part = frames_ref[c * rows:(c + 1) * rows, :].astype(jnp.float32)
            norm[c] = normalize(part, gain_ref[...]).astype(jnp.bfloat16)

            @pl.when(jnp.logical_not(self_kept))
            def _():
                direct(c).start()

            @pl.when(self_kept)
            def _():
                held[b * chunks + c] = norm[c]

    for load in loads[1:]:
        load.start()

    lane = lax.broadcasted_iota(jnp.int32, (rows, 128), 1)
    row = lax.broadcasted_iota(jnp.int32, (rows, 128), 0)
    scale = head_width ** (-0.5) * math.log2(math.e)
    starts = starts_of(lengths_ref)

    for h in range(heads):
        at_row = lax.broadcasted_iota(jnp.int32, (16, v_ref.shape[2]), 0)
        v_ref[h, head_width:, :] = jnp.where(at_row == 0, 1.0, 0.0).astype(jnp.bfloat16)

    def padded(part):
        return jnp.concatenate([part, jnp.zeros((rows, 128 - head_width), jnp.float32)], axis=1)

    def project(u):
        out = jnp.dot(held[u], weights[...], preferred_element_type=jnp.float32)
        seg = seg_at(starts, mine * blocks * chunks * rows + u * rows + row)
        same = lane - head_width == seg
        at = pl.ds(pl.multiple_of(u * rows, rows), rows)
        for h in range(heads):
            o = 3 * head_width * h
            q = padded(out[:, o:o + head_width] * scale)
            k = padded(out[:, o + head_width:o + 2 * head_width])
            v = out[:, o + 2 * head_width:o + 3 * head_width]
            q = jnp.where(lane < head_width, q, jnp.where(same, big_negative, 0.0))
            k = jnp.where(lane < head_width, k, jnp.where(same, 0.0, 1.0))
            q_ref[h, at, :] = q.astype(jnp.bfloat16)
            k_ref[h, at, :] = k.astype(jnp.bfloat16)
            v_ref[h, :head_width, at] = v.T.astype(jnp.bfloat16)

    def pair(u):
        return remote(held.at[u], held.at[u], p_sem.at[u], r_sem.at[u], b, partner)

    def across(u, i):
        other = b - share + (share + i) % np_
        return remote(held.at[u], held.at[u], y_sem.at[u, i], r_sem.at[u], other, g)

    def over(u, k):
        return remote(held.at[u], held.at[u], x_sem.at[u, k], r_sem.at[u], b, 2 * k + core)

    def unit(j, i):
        n = j // chunks
        n = n + place // pairs * (pairs - 1 - 2 * n)
        return ((2 * n + core) * np_ + (share + i) % np_) * chunks + j % chunks

    count = pairs * chunks

    def take(j, carry):
        u = unit(j, 0)

        @pl.when(jnp.logical_not(jnp.logical_and(u // chunks == b, mine == g)))
        def _():
            pair(u).wait_recv()

        for k in range(pairs):
            @pl.when(jnp.logical_and(chip == source_chip, chip != k))
            def _():
                over(u, k).start()

        for i in range(1, np_):
            across(u, i).start()
        pair(u).start()
        return carry

    with jax.named_scope("take"):
        lax.fori_loop(0, count, take, 0)
    loads[0].wait()

    def own(j, carry):
        project(unit(j, 0))
        return carry

    with jax.named_scope("own"):
        lax.fori_loop(0, count, own, 0)

    def pass_on(j, carry):
        for i in range(1, np_):
            u = unit(j, i)
            pair(u).wait_recv()
            pair(u).start()
            project(u)
        return carry

    if np_ > 1:
        with jax.named_scope("pass_on"):
            lax.fori_loop(0, count, pass_on, 0)

    def rest(j, carry):
        n = j // (np_ * chunks)
        n = n + place // pairs * (pairs - 1 - 2 * n)
        i = j // chunks % np_
        u = ((2 * n + 1 - core) * np_ + (share + i) % np_) * chunks + j % chunks
        pair(u).wait_recv()
        project(u)
        return carry

    with jax.named_scope("rest"):
        lax.fori_loop(0, count * np_, rest, 0)

    def send(s):
        return remote(
            mixed_heads.at[s], parts.at[unit_index], s_sem.at[s], a_sem.at[unit_index], s, mine
        )

    def attend_for(i, carry):
        s = (b + 1 + i) % blocks
        at = pl.ds(pl.multiple_of(s * block, block), block)
        mixed_heads[s] = attend(head_width, q_ref, k_ref, v_ref, at)
        kept = jnp.logical_and(home, s == b)

        @pl.when(jnp.logical_not(kept))
        def _():
            send(s).start()

        @pl.when(kept)
        def _():
            parts[unit_index] = mixed_heads[s]

        return carry

    with jax.named_scope("attend"):
        lax.fori_loop(0, blocks, attend_for, 0)

    row = position * block + lax.broadcasted_iota(jnp.int32, (block, 128), 0)
    low = jnp.zeros((block, 128), jnp.int32)
    high = jnp.full((block, 128), blocks * groups * block, jnp.int32)
    for start in starts:
        low = jnp.where(row >= start, jnp.maximum(low, start), low)
        high = jnp.where(row < start, jnp.minimum(high, start), high)
    for t in range(taps):
        at = row + (t - half)
        masks[t] = jnp.where(jnp.logical_and(at >= low, at < high), 1.0, 0.0)

    with jax.named_scope("parts_wait"):
        for i in range(blocks):
            @pl.when(jnp.logical_not(jnp.logical_and(home, unit_index == i)))
            def _():
                remote(parts.at[i], parts.at[i], s_sem.at[i], a_sem.at[i], b, g).wait_recv()

    with jax.named_scope("mid_mm"):
        attended = jnp.concatenate([parts[i] for i in range(blocks)], axis=1)
        loads[1].wait()
        total = frames_ref[...].astype(jnp.float32) + jnp.dot(
            attended, w_out[...], preferred_element_type=jnp.float32
        )
        residual[...] = total.astype(jnp.bfloat16)
        conv_in = normalize(residual[...].astype(jnp.float32), conv_gain_ref[...]).astype(jnp.bfloat16)
        loads[2].wait()
        step = 256
        for n in range(0, width, step):
            a = jnp.dot(conv_in, w_glu[:, n:n + step], preferred_element_type=jnp.float32)
            gate = jnp.dot(
                conv_in, w_glu[:, width + n:width + n + step], preferred_element_type=jnp.float32
            )
            gated = (a * jax.nn.sigmoid(gate)).astype(jnp.bfloat16)
            edge[0, :, n:n + step] = gated[:rim]
            edge[1, :, n:n + step] = gated[block - rim:]
            for c in range(0, step, 128):
                extended[(n + c) // 128, rim:rim + block, :] = gated[:, c:c + 128].astype(jnp.float32)

    after = (position + 1) % (blocks * groups)
    before = (position + blocks * groups - 1) % (blocks * groups)
    to_next = remote(
        edge.at[1], halo.at[0], hs_sem.at[1], hr_sem.at[0], after % blocks, after // blocks
    )
    to_prev = remote(
        edge.at[0], halo.at[1], hs_sem.at[0], hr_sem.at[1], before % blocks, before // blocks
    )
    to_next.start()
    to_prev.start()

    strip = min(64, block)
    spans = -(-taps // 8)

    def convolve(strips):
        def column(c, carry):
            cols = pl.ds(pl.multiple_of(c * 128, 128), 128)
            for r in strips:
                acc = jnp.zeros((strip, 128), jnp.float32)
                for p in range(8):
                    o = rim + r + p - half
                    slab = extended[c, o:o + strip + 8 * (spans - 1), :]
                    for j in range(spans):
                        t = 8 * j + p
                        if t < taps:
                            x = slab[8 * j:8 * j + strip] * masks[t, r:r + strip, :]
                            acc = acc + x * depth_ref[t:t + 1, cols]
                mixed[r:r + strip, cols] = acc
            return carry

        lax.fori_loop(0, width // 128, column, 0)

    every = list(range(0, block, strip))
    with jax.named_scope("conv_mid"):
        convolve(every[1:-1])
    with jax.named_scope("halo_wait"):
        to_next.wait_recv()
        to_prev.wait_recv()
    with jax.named_scope("conv_edge"):
        for c in range(width // 128):
            extended[c, :rim, :] = halo[0, :, 128 * c:128 * c + 128].astype(jnp.float32)
            extended[c, rim + block:2 * rim + block, :] = halo[1, :, 128 * c:128 * c + 128].astype(jnp.float32)
        convolve([every[0], every[-1]])
    with jax.named_scope("tail_mm"):
        normed = normalize(mixed[...], depth_gain_ref[...])
        activated = (normed * jax.nn.sigmoid(normed)).astype(jnp.bfloat16)
        loads[3].wait()
        out_ref[0] = (
            residual[...].astype(jnp.float32)
            + jnp.dot(activated, w_proj[...], preferred_element_type=jnp.float32)
        ).astype(out_ref.dtype)

    for c in range(chunks):
        @pl.when(jnp.logical_not(self_kept))
        def _():
            direct(c).wait_send()

    def drain(j, carry):
        u = unit(j, 0)
        for k in range(pairs):
            @pl.when(jnp.logical_and(chip == source_chip, chip != k))
            def _():
                over(u, k).wait_send()

        for i in range(1, np_):
            across(u, i).wait_send()
        for i in range(np_):
            pair(unit(j, i)).wait_send()
        return carry

    lax.fori_loop(0, count, drain, 0)

    for i in range(blocks):
        @pl.when(jnp.logical_not(jnp.logical_and(home, b == i)))
        def _():
            send(i).wait_send()

    to_next.wait_send()
    to_prev.wait_send()


def attend(head_width, q_ref, k_ref, v_ref, at):
    outs = []
    for h in range(q_ref.shape[0]):
        scores = lax.dot_general(
            k_ref[h], q_ref[h, at, :], (((1,), (1,)), ((), ())),
            preferred_element_type=jnp.float32,
        )
        top = jnp.max(scores, axis=0, keepdims=True)
        weights = jnp.exp2(scores - top).astype(jnp.bfloat16)
        mixed = jnp.dot(v_ref[h], weights, preferred_element_type=jnp.float32)
        outs.append(mixed[:head_width] / mixed[head_width:head_width + 1])
    return jnp.concatenate(outs, axis=0).T.astype(jnp.bfloat16)


def body(
    frames, utt_lengths, attn_gain, w_qkv, w_out, conv_gain, w_glu, w_depth, depth_gain, w_proj
):
    rows, width = frames.shape[1:]
    blocks, groups = lax.axis_size("blk"), lax.axis_size("grp")
    head_width = width // HEADS
    np_ = blocks // groups
    columns = w_qkv.shape[1] // np_
    heads = columns // (3 * head_width)
    window = rows * blocks
    chunks = 2 if rows % 32 == 0 else 1
    taps = w_depth.shape[0]
    rim = -(-(taps // 2) // 16) * 16
    vm = pl.BlockSpec(memory_space=pltpu.VMEM)
    hbm = pl.BlockSpec(memory_space=pl.ANY)
    return pl.pallas_call(
        functools.partial(block_kernel, blocks, groups, chunks, head_width),
        out_shape=jax.ShapeDtypeStruct((1, rows, width), jnp.bfloat16),
        in_specs=[pl.BlockSpec(memory_space=pltpu.SMEM)] + [vm] * 5 + [hbm] * 4,
        out_specs=vm,
        scratch_shapes=[
            pltpu.VMEM((chunks, rows // chunks, width), jnp.bfloat16),
            pltpu.VMEM((blocks * chunks, rows // chunks, width), jnp.bfloat16),
            pltpu.VMEM((width, columns), jnp.bfloat16),
            pltpu.VMEM((heads, window, 128), jnp.bfloat16),
            pltpu.VMEM((heads, window, 128), jnp.bfloat16),
            pltpu.VMEM((heads, head_width + 16, window), jnp.bfloat16),
            pltpu.VMEM((blocks, rows, heads * head_width), jnp.bfloat16),
            pltpu.VMEM((blocks, rows, heads * head_width), jnp.bfloat16),
            pltpu.VMEM(w_out.shape, jnp.bfloat16),
            pltpu.VMEM(w_glu.shape, jnp.bfloat16),
            pltpu.VMEM(w_proj.shape, jnp.bfloat16),
            pltpu.VMEM((taps, rows, 128), jnp.float32),
            pltpu.VMEM((rows, width), jnp.bfloat16),
            pltpu.VMEM((2, rim, width), jnp.bfloat16),
            pltpu.VMEM((2, rim, width), jnp.bfloat16),
            pltpu.VMEM((width // 128, rows + 2 * rim + 8, 128), jnp.float32),
            pltpu.VMEM((rows, width), jnp.float32),
            pltpu.SemaphoreType.DMA((4,)),
            pltpu.SemaphoreType.DMA((chunks,)),
            pltpu.SemaphoreType.DMA((blocks * chunks, groups // 2)),
            pltpu.SemaphoreType.DMA((blocks * chunks, np_)),
            pltpu.SemaphoreType.DMA((blocks * chunks,)),
            pltpu.SemaphoreType.DMA((blocks * chunks,)),
            pltpu.SemaphoreType.DMA((blocks,)),
            pltpu.SemaphoreType.DMA((blocks,)),
            pltpu.SemaphoreType.DMA((2,)),
            pltpu.SemaphoreType.DMA((2,)),
        ],
        compiler_params=pltpu.CompilerParams(has_side_effects=True, vmem_limit_bytes=VMEM_LIMIT),
        name="block",
    )(
        utt_lengths, frames[0], attn_gain[None], conv_gain[None], w_depth, depth_gain[None],
        w_qkv, w_out, w_glu, w_proj,
    )


def solution(mesh):
    in_specs = (P("grp", "blk", None), P(), P(), P(None, "grp"), P(), P(), P(), P(), P(), P())
    out_specs = P("grp", "blk", None)
    return jax.shard_map(body, mesh=mesh, in_specs=in_specs, out_specs=out_specs, check_vma=False)
```

time: 91.9 us -> 87.3 us (0.950)
  Pallas kernels: 89.9 us -> 85.3 us
    pallas_call x2 -> x1, Pallas kernels: 89.9 us -> 85.3 us  [body(): pl.pallas_call(functools.partial(block_kernel, blocks, groups, chunks, he...]
where the time goes in v1:
time: 87.3 us; the launch traced here: 87.2 us
  Pallas kernels  85.3 us (98%)
  local copies, waits for them, and re-layouts  1.87 us (2%)
    pallas_call x1, Pallas kernels, body(): pl.pallas_call(functools.partial(block_kernel, blocks, groups, chunks, he...  85.3 us
    unnamed x1, local copies, waits for them, and re-layouts  1.87 us

profile of v1, /device:TPU:0, one launch (start us, length us, event | category | flops | bytes accessed | tf_op | source)
XLA Modules:
  0.0 87.2 jit_solution(14384480081729597584)
XLA Ops:
  0.0 85.3 %block.1 = bf16[1,256,1024]{2,1,0:T(8,128)(2,1)} custom-call(s32[4]{0:T(128)} %lengths_ref.1, bf16[256,1024]{1,0:T(8,128)(2,1)} %bitcast.4, f32[1,1024]{1,0:T(1,128)} %bitcast.5, f32[1,1024]{1,0:T(1,128)} %bitcast.6, f32[31,1024]{1,0:T(8,128)} %depth_ref.1, f32[1,1024]{1,0:T(1,128)} %bitcast.7, bf16[1024,768]{1,0:T(8,128)(2,1)} %w_ref.1, ...), custom_call_target="tpu_custom_call" | custom-call | tf_op jit(solution)/shard_map/block/pallas_call | solution.py:386
  85.3 1.9 %copy.12 = bf16[1,256,1024]{2,1,0:T(8,128)(2,1)} copy(bf16[1,256,1024]{2,1,0:T(8,128)(2,1)} %block.1) | data formatting | bytes 1048576

commit v2 on v1

v2 whole, which is shorter than its diff:
```python
import functools
import math

import jax
import jax.numpy as jnp
from jax import lax
from jax.experimental import pallas as pl
from jax.experimental.pallas import tpu as pltpu
from jax.sharding import PartitionSpec as P

HEADS = 16

epsilon = 1e-05
big_negative = -1e30
MESH = pl.DeviceIdType.MESH
VMEM_LIMIT = 56 * 1024 * 1024


def normalize(values, row_gain):
    center = values - jnp.mean(values, axis=-1, keepdims=True)
    spread = jnp.mean(center * center, axis=-1, keepdims=True)
    return center * lax.rsqrt(spread + epsilon) * row_gain


def starts_of(lengths_ref):
    starts, total = [], jnp.int32(0)
    for c in range(lengths_ref.shape[0]):
        starts.append(total)
        total = total + lengths_ref[c]
    return starts


def seg_at(starts, positions):
    seg = jnp.full(positions.shape, -1, jnp.int32)
    for start in starts:
        seg = seg + jnp.where(positions >= start, 1, 0)
    return seg


def remote(src, dst, send, recv, blk, grp):
    return pltpu.make_async_remote_copy(
        src_ref=src, dst_ref=dst, send_sem=send, recv_sem=recv,
        device_id=(blk, grp), device_id_type=MESH,
    )


def slot_of(b, g, blocks):
    half = blocks // 2
    return (b % half + (g % 2 + g // 2) * half) % blocks


def block_kernel(
    blocks, groups, parts_of_chunk, head_width,
    lengths_ref, frames_in, gain_in, conv_gain_in, depth_in, depth_gain_in,
    w_ref, w_out_ref, w_glu_ref, w_proj_ref,
    out_ref,
    frames_ref, gain_ref, conv_gain_ref, depth_ref, depth_gain_ref, norm, held, weights, lent, q_ref, k_ref, v_ref, scores,
    mixed_heads, parts, w_out, w_glu, w_proj, masks, residual, edge, halo, extended, mixed,
    load_sem, in_sem, ws_sem, wr_sem, d_sem, x_sem, y_sem, p_sem, r_sem, s_sem, a_sem, hs_sem, hr_sem,
):
    b, g = lax.axis_index("blk"), lax.axis_index("grp")
    np_ = blocks // groups
    steps = blocks // np_
    reach = steps // 2
    rows, width = held.shape[1:]
    chunks = norm.shape[0]
    block = rows * chunks
    part_rows = rows // parts_of_chunk
    columns = weights.shape[1]
    heads = columns // (3 * head_width)
    taps = depth_ref.shape[0]
    half = (taps - 1) // 2
    rim = halo.shape[1]
    step, share, core, chip = b // np_, b % np_, g % 2, g // 2
    side = step // reach
    mine = 2 * chip + side
    partner = g + 1 - 2 * core
    slot = slot_of(b, g, blocks)
    home = mine == g
    position = g * blocks + b

    after = (position + 1) % (blocks * groups)
    before = (position + blocks * groups - 1) % (blocks * groups)
    barrier = pltpu.get_barrier_semaphore()

    def hail(other_b, other_g):
        pl.semaphore_signal(
            barrier, inc=1, device_id=(other_b, other_g), device_id_type=MESH
        )

    for c in range(2):
        def hail_row(i, carry):
            @pl.when(jnp.logical_or(i != b, core != c))
            def _():
                hail(i, 2 * chip + c)

            return carry

        lax.fori_loop(0, blocks, hail_row, 0)
    for other in range(groups):
        @pl.when(chip != other // 2)
        def _():
            hail(b, other)

    callers = 2 * blocks - 1 + groups - 2
    for near in (after, before):
        apart = near // blocks // 2 != chip

        @pl.when(apart)
        def _():
            hail(near % blocks, near // blocks)

        callers = callers + jnp.where(apart, 1, 0)

    inputs = [
        pltpu.make_async_copy(src, dst, in_sem.at[i]) for i, (src, dst) in enumerate([
            (frames_in, frames_ref), (gain_in, gain_ref), (conv_gain_in, conv_gain_ref),
            (depth_in, depth_ref), (depth_gain_in, depth_gain_ref),
        ])
    ]
    for copy in inputs:
        copy.start()

    def slab_of(sub):
        if np_ == 1:
            return w_ref
        return w_ref.at[:, pl.ds(pl.multiple_of(sub * columns, 128), columns)]

    own_slab = slot // np_ == g
    load_own = pltpu.make_async_copy(slab_of(b % np_), weights, load_sem.at[0])
    load_lent = pltpu.make_async_copy(slab_of(b % np_), lent, load_sem.at[4])

    def give(other):
        return slot_of(b, other, blocks) // np_, remote(
            lent, weights, ws_sem.at[other], wr_sem.at[0], b, other
        )

    @pl.when(own_slab)
    def _():
        load_own.start()

    load_lent.start()

    loads = [
        pltpu.make_async_copy(w_out_ref, w_out, load_sem.at[1]),
        pltpu.make_async_copy(w_glu_ref, w_glu, load_sem.at[2]),
        pltpu.make_async_copy(w_proj_ref, w_proj, load_sem.at[3]),
    ]

    def entry(n, at_side):
        first = at_side * reach
        return jnp.clip(n, first, first + reach - 1)

    target = entry(step, core) * np_ + share
    target_core = step % 2
    self_kept = jnp.logical_and(target == b, target_core == core)

    def piece(ref, u, k):
        return ref.at[u, pl.ds(k * part_rows, part_rows)]

    def direct(c, k):
        u = b * chunks + c
        return remote(
            piece(norm, c, k), piece(held, u, k), d_sem.at[c * parts_of_chunk + k], r_sem.at[u * parts_of_chunk + k],
            target, 2 * chip + target_core,
        )

    with jax.named_scope("in_wait"):
        for copy in inputs:
            copy.wait()
    with jax.named_scope("norm"):
        for c in range(chunks):
            part = frames_ref[c * rows:(c + 1) * rows, :].astype(jnp.float32)
            norm[c] = normalize(part, gain_ref[...]).astype(jnp.bfloat16)
    with jax.named_scope("barrier"):
        pl.semaphore_wait(barrier, callers)
    for c in range(chunks):
        for k in range(parts_of_chunk):
            at = slice(k * part_rows, (k + 1) * part_rows)

            @pl.when(jnp.logical_not(self_kept))
            def _():
                direct(c, k).start()

            @pl.when(self_kept)
            def _():
                held[b * chunks + c, at] = norm[c, at]

    load_lent.wait()
    for other in range(groups):
        source, copy = give(other)

        @pl.when(jnp.logical_and(source == g, other != g))
        def _():
            copy.start()

    for load in loads:
        load.start()

    lane = lax.broadcasted_iota(jnp.int32, (rows, 128), 1)
    row = lax.broadcasted_iota(jnp.int32, (rows, 128), 0)
    scale = head_width ** (-0.5) * math.log2(math.e)
    starts = starts_of(lengths_ref)

    for h in range(heads):
        at_row = lax.broadcasted_iota(jnp.int32, (16, v_ref.shape[2]), 0)
        v_ref[h, head_width:, :] = jnp.where(at_row == 0, 1.0, 0.0).astype(jnp.bfloat16)

    def padded(part):
        return jnp.concatenate([part, jnp.zeros((rows, 128 - head_width), jnp.float32)], axis=1)

    def project(u):
        out = jnp.dot(held[u], weights[...], preferred_element_type=jnp.float32)
        seg = seg_at(starts, mine * blocks * chunks * rows + u * rows + row)
        same = lane - head_width == seg
        at = pl.ds(pl.multiple_of(u * rows, rows), rows)
        for h in range(heads):
            o = 3 * head_width * h
            q = padded(out[:, o:o + head_width] * scale)
            k = padded(out[:, o + head_width:o + 2 * head_width])
            v = out[:, o + 2 * head_width:o + 3 * head_width]
            q = jnp.where(lane < head_width, q, jnp.where(same, big_negative, 0.0))
            k = jnp.where(lane < head_width, k, jnp.where(same, 0.0, 1.0))
            q_ref[h, at, :] = q.astype(jnp.bfloat16)
            k_ref[h, at, :] = k.astype(jnp.bfloat16)
            v_ref[h, :head_width, at] = v.T.astype(jnp.bfloat16)

    def pair(u, k):
        return remote(
            piece(held, u, k), piece(held, u, k), p_sem.at[u * parts_of_chunk + k], r_sem.at[u * parts_of_chunk + k], b, partner
        )

    def across(u, i, k):
        other = b - share + (share + i) % np_
        return remote(
            piece(held, u, k), piece(held, u, k), y_sem.at[(u * np_ + i) * parts_of_chunk + k], r_sem.at[u * parts_of_chunk + k], other, g
        )

    def over(u, i, k):
        other = side * reach + i
        return remote(
            piece(held, u, k), piece(held, u, k), x_sem.at[(u * reach + i) * parts_of_chunk + k], r_sem.at[u * parts_of_chunk + k],
            other * np_ + share, g,
        )

    def unit(j, i, parity):
        n = j // chunks
        n = n + side * (reach - 1 - 2 * n)
        return ((2 * n + parity) * np_ + (share + i) % np_) * chunks + j % chunks

    count = reach * chunks

    def enters(u):
        return entry(u // (chunks * np_), side) == step

    def take(j):
        u = unit(j, 0, core)
        for k in range(parts_of_chunk):
            @pl.when(jnp.logical_not(jnp.logical_and(u // chunks == b, home)))
            def _():
                pair(u, k).wait_recv()

            for i in range(reach):
                @pl.when(enters(u) & (step != side * reach + i))
                def _():
                    over(u, i, k).start()

            for i in range(1, np_):
                across(u, i, k).start()
            pair(u, k).start()

    def arrive(u):
        for k in range(parts_of_chunk):
            pair(u, k).wait_recv()

    def pass_on(j):
        for i in range(1, np_):
            u = unit(j, i, core)
            for k in range(parts_of_chunk):
                pair(u, k).wait_recv()
                pair(u, k).start()

    with jax.named_scope("first"):
        take(0)
        take(1)
        pass_on(0)

    with jax.named_scope("weights"):
        @pl.when(own_slab)
        def _():
            load_own.wait()

        @pl.when(jnp.logical_not(own_slab))
        def _():
            give(0)[1].wait_recv()

    def gather(j, carry):
        project(unit(j, 0, core))
        u = unit(j, 0, 1 - core)
        arrive(u)
        project(u)

        @pl.when(j + 2 < count)
        def _():
            take(j + 2)

        for i in range(1, np_):
            project(unit(j, i, core))

        @pl.when(j + 1 < count)
        def _():
            pass_on(j + 1)

        for i in range(1, np_):
            u = unit(j, i, 1 - core)
            arrive(u)
            project(u)
        return carry

    with jax.named_scope("gather"):
        lax.fori_loop(0, count, gather, 0)

    def send(s):
        return remote(
            mixed_heads.at[s], parts.at[slot], s_sem.at[s], a_sem.at[slot], s, mine
        )

    tile = min(512, blocks * block)
    tiles = blocks * block // tile

    def order(i):
        return (b + 1 + i) % blocks

    def score(i, h, n, top):
        at = pl.ds(pl.multiple_of(order(i) * block, block), block)
        keys = slice(n * tile, (n + 1) * tile)
        raw = lax.dot_general(
            k_ref[h, keys, :], q_ref[h, at, :], (((1,), (1,)), ((), ())),
            preferred_element_type=jnp.float32,
        )
        scores[h, keys, :] = raw
        return jnp.maximum(top, jnp.max(raw.reshape(tile // 8, 8, block), axis=0))

    def mix(h, n, top, total):
        keys = slice(n * tile, (n + 1) * tile)
        probs = jnp.exp2(scores[h, keys, :] - top).astype(jnp.bfloat16)
        return total + jnp.dot(v_ref[h, :, keys], probs, preferred_element_type=jnp.float32)

    lowest = jnp.full((8, block), -jnp.inf, jnp.float32)

    def attend_for(i, top):
        outs = []
        for h in range(heads):
            top = jnp.max(top, axis=0, keepdims=True)
            later = lowest
            total = jnp.zeros((v_ref.shape[1], block), jnp.float32)
            next_i, next_h = (i, h + 1) if h + 1 < heads else (jnp.minimum(i + 1, blocks - 1), 0)
            if heads == 1:
                for n in range(tiles):
                    total = mix(h, n, top, total)
                for n in range(tiles):
                    later = score(next_i, next_h, n, later)
            else:
                for n in range(tiles):
                    later = score(next_i, next_h, n, later)
                    total = mix(h, n, top, total)
            outs.append(total[:head_width] / total[head_width:head_width + 1])
            top = later
        s = order(i)
        mixed_heads[s] = jnp.concatenate(outs, axis=0).T.astype(jnp.bfloat16)
        kept = jnp.logical_and(home, s == b)

        @pl.when(jnp.logical_not(kept))
        def _():
            send(s).start()

        @pl.when(kept)
        def _():
            parts[slot] = mixed_heads[s]

        return top

    with jax.named_scope("attend"):
        top = lowest
        for n in range(tiles):
            top = score(0, 0, n, top)
        lax.fori_loop(0, blocks, attend_for, top)

    row = position * block + lax.broadcasted_iota(jnp.int32, (block, 128), 0)
    low = jnp.zeros((block, 128), jnp.int32)
    high = jnp.full((block, 128), blocks * groups * block, jnp.int32)
    for start in starts:
        low = jnp.where(row >= start, jnp.maximum(low, start), low)
        high = jnp.where(row < start, jnp.minimum(high, start), high)
    for t in range(taps):
        at = row + (t - half)
        masks[t] = jnp.where(jnp.logical_and(at >= low, at < high), 1.0, 0.0)

    with jax.named_scope("parts_wait"):
        for i in range(blocks):
            @pl.when(jnp.logical_not(jnp.logical_and(home, slot == i)))
            def _():
                remote(parts.at[i], parts.at[i], s_sem.at[i], a_sem.at[i], b, g).wait_recv()

    with jax.named_scope("mid_mm"):
        attended = jnp.concatenate([parts[i] for i in range(blocks)], axis=1)
        loads[0].wait()
        total = frames_ref[...].astype(jnp.float32) + jnp.dot(
            attended, w_out[...], preferred_element_type=jnp.float32
        )
        residual[...] = total.astype(jnp.bfloat16)
        conv_in = normalize(residual[...].astype(jnp.float32), conv_gain_ref[...]).astype(jnp.bfloat16)
        loads[1].wait()
        span = 256
        for n in range(0, width, span):
            a = jnp.dot(conv_in, w_glu[:, n:n + span], preferred_element_type=jnp.float32)
            gate = jnp.dot(
                conv_in, w_glu[:, width + n:width + n + span], preferred_element_type=jnp.float32
            )
            gated = (a * jax.nn.sigmoid(gate)).astype(jnp.bfloat16)
            edge[0, :, n:n + span] = gated[:rim]
            edge[1, :, n:n + span] = gated[block - rim:]
            for c in range(0, span, 128):
                extended[(n + c) // 128, rim:rim + block, :] = gated[:, c:c + 128].astype(jnp.float32)

    to_next = remote(
        edge.at[1], halo.at[0], hs_sem.at[1], hr_sem.at[0], after % blocks, after // blocks
    )
    to_prev = remote(
        edge.at[0], halo.at[1], hs_sem.at[0], hr_sem.at[1], before % blocks, before // blocks
    )
    to_next.start()
    to_prev.start()

    strip = min(64, block)
    spans = -(-taps // 8)

    def convolve(strips):
        def column(c, carry):
            cols = pl.ds(pl.multiple_of(c * 128, 128), 128)
            for r in strips:
                acc = jnp.zeros((strip, 128), jnp.float32)
                for p in range(8):
                    o = rim + r + p - half
                    slab = extended[c, o:o + strip + 8 * (spans - 1), :]
                    for j in range(spans):
                        t = 8 * j + p
                        if t < taps:
                            x = slab[8 * j:8 * j + strip] * masks[t, r:r + strip, :]
                            acc = acc + x * depth_ref[t:t + 1, cols]
                mixed[r:r + strip, cols] = acc
            return carry

        lax.fori_loop(0, width // 128, column, 0)

    every = list(range(0, block, strip))
    with jax.named_scope("conv_mid"):
        convolve(every[1:-1])
    with jax.named_scope("halo_wait"):
        to_next.wait_recv()
        to_prev.wait_recv()
    with jax.named_scope("conv_edge"):
        for c in range(width // 128):
            extended[c, :rim, :] = halo[0, :, 128 * c:128 * c + 128].astype(jnp.float32)
            extended[c, rim + block:2 * rim + block, :] = halo[1, :, 128 * c:128 * c + 128].astype(jnp.float32)
        convolve([every[0], every[-1]])
    with jax.named_scope("tail_mm"):
        normed = normalize(mixed[...], depth_gain_ref[...])
        activated = (normed * jax.nn.sigmoid(normed)).astype(jnp.bfloat16)
        loads[2].wait()
        out_ref[0] = (
            residual[...].astype(jnp.float32)
            + jnp.dot(activated, w_proj[...], preferred_element_type=jnp.float32)
        ).astype(out_ref.dtype)

    with jax.named_scope("drain"):
        for c in range(chunks):
            for k in range(parts_of_chunk):
                @pl.when(jnp.logical_not(self_kept))
                def _():
                    direct(c, k).wait_send()

        for other in range(groups):
            source, copy = give(other)

            @pl.when(jnp.logical_and(source == g, other != g))
            def _():
                copy.wait_send()

        def drain(j, carry):
            u = unit(j, 0, core)
            for k in range(parts_of_chunk):
                for i in range(reach):
                    @pl.when(enters(u) & (step != side * reach + i))
                    def _():
                        over(u, i, k).wait_send()

                for i in range(1, np_):
                    across(u, i, k).wait_send()
                for i in range(np_):
                    pair(unit(j, i, core), k).wait_send()
            return carry

        lax.fori_loop(0, count, drain, 0)

        for i in range(blocks):
            @pl.when(jnp.logical_not(jnp.logical_and(home, b == i)))
            def _():
                send(i).wait_send()

        to_next.wait_send()
        to_prev.wait_send()


def body(
    frames, utt_lengths, attn_gain, w_qkv, w_out, conv_gain, w_glu, w_depth, depth_gain, w_proj
):
    rows, width = frames.shape[1:]
    blocks, groups = lax.axis_size("blk"), lax.axis_size("grp")
    head_width = width // HEADS
    np_ = blocks // groups
    columns = w_qkv.shape[1] // np_
    heads = columns // (3 * head_width)
    window = rows * blocks
    chunks = 2 if rows % 32 == 0 else 1
    parts_of_chunk = 2 if rows // chunks % 32 == 0 else 1
    reach = blocks // np_ // 2
    taps = w_depth.shape[0]
    rim = -(-(taps // 2) // 16) * 16
    vm = pl.BlockSpec(memory_space=pltpu.VMEM)
    hbm = pl.BlockSpec(memory_space=pl.ANY)
    return pl.pallas_call(
        functools.partial(block_kernel, blocks, groups, parts_of_chunk, head_width),
        out_shape=jax.ShapeDtypeStruct((1, rows, width), jnp.bfloat16),
        in_specs=[pl.BlockSpec(memory_space=pltpu.SMEM)] + [hbm] * 9,
        out_specs=vm,
        scratch_shapes=[
            pltpu.VMEM((rows, width), jnp.bfloat16),
            pltpu.VMEM((1, width), jnp.float32),
            pltpu.VMEM((1, width), jnp.float32),
            pltpu.VMEM(w_depth.shape, jnp.float32),
            pltpu.VMEM((1, width), jnp.float32),
            pltpu.VMEM((chunks, rows // chunks, width), jnp.bfloat16),
            pltpu.VMEM((blocks * chunks, rows // chunks, width), jnp.bfloat16),
            pltpu.VMEM((width, columns), jnp.bfloat16),
            pltpu.VMEM((width, columns), jnp.bfloat16),
            pltpu.VMEM((heads, window, 128), jnp.bfloat16),
            pltpu.VMEM((heads, window, 128), jnp.bfloat16),
            pltpu.VMEM((heads, head_width + 16, window), jnp.bfloat16),
            pltpu.VMEM((heads, window, rows), jnp.float32),
            pltpu.VMEM((blocks, rows, heads * head_width), jnp.bfloat16),
            pltpu.VMEM((blocks, rows, heads * head_width), jnp.bfloat16),
            pltpu.VMEM(w_out.shape, jnp.bfloat16),
            pltpu.VMEM(w_glu.shape, jnp.bfloat16),
            pltpu.VMEM(w_proj.shape, jnp.bfloat16),
            pltpu.VMEM((taps, rows, 128), jnp.float32),
            pltpu.VMEM((rows, width), jnp.bfloat16),
            pltpu.VMEM((2, rim, width), jnp.bfloat16),
            pltpu.VMEM((2, rim, width), jnp.bfloat16),
            pltpu.VMEM((width // 128, rows + 2 * rim + 8, 128), jnp.float32),
            pltpu.VMEM((rows, width), jnp.float32),
            pltpu.SemaphoreType.DMA((5,)),
            pltpu.SemaphoreType.DMA((5,)),
            pltpu.SemaphoreType.DMA((groups,)),
            pltpu.SemaphoreType.DMA((1,)),
            pltpu.SemaphoreType.DMA((chunks * parts_of_chunk,)),
            pltpu.SemaphoreType.DMA((blocks * chunks * reach * parts_of_chunk,)),
            pltpu.SemaphoreType.DMA((blocks * chunks * np_ * parts_of_chunk,)),
            pltpu.SemaphoreType.DMA((blocks * chunks * parts_of_chunk,)),
            pltpu.SemaphoreType.DMA((blocks * chunks * parts_of_chunk,)),
            pltpu.SemaphoreType.DMA((blocks,)),
            pltpu.SemaphoreType.DMA((blocks,)),
            pltpu.SemaphoreType.DMA((2,)),
            pltpu.SemaphoreType.DMA((2,)),
        ],
        compiler_params=pltpu.CompilerParams(
            collective_id=0, has_side_effects=True, vmem_limit_bytes=VMEM_LIMIT),
        name="block",
    )(
        utt_lengths, frames[0], attn_gain[None], conv_gain[None], w_depth, depth_gain[None],
        w_qkv, w_out, w_glu, w_proj,
    )


def solution(mesh):
    in_specs = (P("grp", "blk", None), P(), P(), P(None, "grp"), P(), P(), P(), P(), P(), P())
    out_specs = P("grp", "blk", None)
    return jax.shard_map(body, mesh=mesh, in_specs=in_specs, out_specs=out_specs, check_vma=False)
```

time: 87.3 us -> 68.2 us (0.78)
  the two profiles are of different devices: /device:TPU:0 before, /device:TPU:1 now
where the time goes in v2:
time: 68.2 us; the launch traced here: 68 us
  Pallas kernels  66.1 us (97%)
  local copies, waits for them, and re-layouts  1.87 us (3%)
    pallas_call x1, Pallas kernels, body(): pl.pallas_call(functools.partial(block_kernel, blocks, groups, parts_of_c...  66.1 us
    unnamed x1, local copies, waits for them, and re-layouts  1.87 us

profile of v2, /device:TPU:1, one launch (start us, length us, event | category | flops | bytes accessed | tf_op | source)
XLA Modules:
  0.0 68.0 jit_solution(11575666751047238153)
XLA Ops:
  0.0 66.1 %block.1 = bf16[1,256,1024]{2,1,0:T(8,128)(2,1)} custom-call(s32[4]{0:T(128)} %lengths_ref.1, bf16[256,1024]{1,0:T(8,128)(2,1)} %bitcast.4, f32[1,1024]{1,0:T(1,128)} %bitcast.5, f32[1,1024]{1,0:T(1,128)} %bitcast.6, f32[31,1024]{1,0:T(8,128)} %depth_in.1, f32[1,1024]{1,0:T(1,128)} %bitcast.7, bf16[1024,768]{1,0:T(8,128)(2,1)} %w_ref.1, ...), custom_call_target="tpu_custom_call" | custom-call | tf_op jit(solution)/shard_map/block/pallas_call | solution.py:532
  66.1 1.9 %copy.12 = bf16[1,256,1024]{2,1,0:T(8,128)(2,1)} copy(bf16[1,256,1024]{2,1,0:T(8,128)(2,1)} %block.1) | data formatting | bytes 1048576

commit v3 on v2

--- a/solution.py
+++ b/solution.py
@@ -225,65 +225,77 @@
             k_ref[h, at, :] = k.astype(jnp.bfloat16)
             v_ref[h, :head_width, at] = v.T.astype(jnp.bfloat16)
 
-    def pair(u, k):
-        return remote(
-            piece(held, u, k), piece(held, u, k), p_sem.at[u * parts_of_chunk + k], r_sem.at[u * parts_of_chunk + k], b, partner
-        )
-
-    def across(u, i, k):
-        other = b - share + (share + i) % np_
-        return remote(
-            piece(held, u, k), piece(held, u, k), y_sem.at[(u * np_ + i) * parts_of_chunk + k], r_sem.at[u * parts_of_chunk + k], other, g
-        )
-
-    def over(u, i, k):
-        other = side * reach + i
-        return remote(
-            piece(held, u, k), piece(held, u, k), x_sem.at[(u * reach + i) * parts_of_chunk + k], r_sem.at[u * parts_of_chunk + k],
-            other * np_ + share, g,
-        )
-
     def unit(j, i, parity):
         n = j // chunks
         n = n + side * (reach - 1 - 2 * n)
         return ((2 * n + parity) * np_ + (share + i) % np_) * chunks + j % chunks
 
+    def came(u, k):
+        here = piece(held, u, k)
+        return remote(here, here, p_sem.at[0], r_sem.at[u * parts_of_chunk + k], b, partner)
+
+    def pair(j, i, k):
+        u = unit(j, i, core)
+        here = piece(held, u, k)
+        return remote(
+            here, here, p_sem.at[(j * np_ + i) * parts_of_chunk + k],
+            r_sem.at[u * parts_of_chunk + k], b, partner,
+        )
+
+    def across(j, i, k):
+        u = unit(j, 0, core)
+        here = piece(held, u, k)
+        return remote(
+            here, here, y_sem.at[(j * np_ + i - 1) * parts_of_chunk + k],
+            r_sem.at[u * parts_of_chunk + k], b - share + (share + i) % np_, g,
+        )
+
+    def over(j, i, k):
+        u = unit(j, 0, core)
+        here = piece(held, u, k)
+        other = side * reach + (step - side * reach + i) % reach
+        return remote(
+            here, here, x_sem.at[(j * (reach - 1) + i - 1) * parts_of_chunk + k],
+            r_sem.at[u * parts_of_chunk + k], other * np_ + share, g,
+        )
+
     count = reach * chunks
 
-    def enters(u):
-        return entry(u // (chunks * np_), side) == step
+    def enters(j):
+        return entry(unit(j, 0, core) // (chunks * np_), side) == step
 
     def take(j):
         u = unit(j, 0, core)
         for k in range(parts_of_chunk):
             @pl.when(jnp.logical_not(jnp.logical_and(u // chunks == b, home)))
             def _():
-                pair(u, k).wait_recv()
-
-            for i in range(reach):
-                @pl.when(enters(u) & (step != side * reach + i))
-                def _():
-                    over(u, i, k).start()
+                came(u, k).wait_recv()
+
+            @pl.when(enters(j))
+            def _():
+                for i in range(1, reach):
+                    over(j, i, k).start()
 
             for i in range(1, np_):
-                across(u, i, k).start()
-            pair(u, k).start()
+                across(j, i, k).start()
+            pair(j, 0, k).start()
 
     def arrive(u):
         for k in range(parts_of_chunk):
-            pair(u, k).wait_recv()
+            came(u, k).wait_recv()
 
     def pass_on(j):
         for i in range(1, np_):
-            u = unit(j, i, core)
             for k in range(parts_of_chunk):
-                pair(u, k).wait_recv()
-                pair(u, k).start()
+                came(unit(j, i, core), k).wait_recv()
+                pair(j, i, k).start()
 
     with jax.named_scope("first"):
         take(0)
         take(1)
         pass_on(0)
+        if count > 2:
+            take(2)
 
     with jax.named_scope("weights"):
         @pl.when(own_slab)
@@ -296,21 +308,20 @@
 
     def gather(j, carry):
         project(unit(j, 0, core))
+
+        @pl.when(j + 3 < count)
+        def _():
+            take(j + 3)
+
+        @pl.when(j >= 1)
+        def _():
+            pass_on(j)
+
         u = unit(j, 0, 1 - core)
         arrive(u)
         project(u)
-
-        @pl.when(j + 2 < count)
-        def _():
-            take(j + 2)
-
         for i in range(1, np_):
             project(unit(j, i, core))
-
-        @pl.when(j + 1 < count)
-        def _():
-            pass_on(j + 1)
-
         for i in range(1, np_):
             u = unit(j, i, 1 - core)
             arrive(u)
@@ -329,7 +340,9 @@
     tiles = blocks * block // tile
 
     def order(i):
-        return (b + 1 + i) % blocks
+        n = i // np_
+        n = side * n + (1 - side) * (steps - 1 - n)
+        return n * np_ + (share + 1 + i) % np_
 
     def score(i, h, n, top):
         at = pl.ds(pl.multiple_of(order(i) * block, block), block)
@@ -488,17 +501,16 @@
                 copy.wait_send()
 
         def drain(j, carry):
-            u = unit(j, 0, core)
             for k in range(parts_of_chunk):
-                for i in range(reach):
-                    @pl.when(enters(u) & (step != side * reach + i))
-                    def _():
-                        over(u, i, k).wait_send()
+                @pl.when(enters(j))
+                def _():
+                    for i in range(1, reach):
+                        over(j, i, k).wait_send()
 
                 for i in range(1, np_):
-                    across(u, i, k).wait_send()
+                    across(j, i, k).wait_send()
                 for i in range(np_):
-                    pair(unit(j, i, core), k).wait_send()
+                    pair(j, i, k).wait_send()
             return carry
 
         lax.fori_loop(0, count, drain, 0)
@@ -564,9 +576,9 @@
             pltpu.SemaphoreType.DMA((groups,)),
             pltpu.SemaphoreType.DMA((1,)),
             pltpu.SemaphoreType.DMA((chunks * parts_of_chunk,)),
-            pltpu.SemaphoreType.DMA((blocks * chunks * reach * parts_of_chunk,)),
-            pltpu.SemaphoreType.DMA((blocks * chunks * np_ * parts_of_chunk,)),
-            pltpu.SemaphoreType.DMA((blocks * chunks * parts_of_chunk,)),
+            pltpu.SemaphoreType.DMA((reach * chunks * (reach - 1) * parts_of_chunk,)),
+            pltpu.SemaphoreType.DMA((reach * chunks * np_ * parts_of_chunk,)),
+            pltpu.SemaphoreType.DMA((reach * chunks * np_ * parts_of_chunk,)),
             pltpu.SemaphoreType.DMA((blocks * chunks * parts_of_chunk,)),
             pltpu.SemaphoreType.DMA((blocks,)),
             pltpu.SemaphoreType.DMA((blocks,)),

time: 68.2 us -> 61.4 us (0.900)
  the two profiles are of different devices: /device:TPU:1 before, /device:TPU:0 now
where the time goes in v3:
time: 61.4 us; the launch traced here: 61.2 us
  Pallas kernels  59.3 us (97%)
  local copies, waits for them, and re-layouts  1.87 us (3%)
    pallas_call x1, Pallas kernels, body(): pl.pallas_call(functools.partial(block_kernel, blocks, groups, parts_of_c...  59.3 us
    unnamed x1, local copies, waits for them, and re-layouts  1.87 us

profile of v3, /device:TPU:0, one launch (start us, length us, event | category | flops | bytes accessed | tf_op | source)
XLA Modules:
  0.0 61.2 jit_solution(15845564488837529607)
XLA Ops:
  0.0 59.3 %block.1 = bf16[1,256,1024]{2,1,0:T(8,128)(2,1)} custom-call(s32[4]{0:T(128)} %lengths_ref.1, bf16[256,1024]{1,0:T(8,128)(2,1)} %bitcast.4, f32[1,1024]{1,0:T(1,128)} %bitcast.5, f32[1,1024]{1,0:T(1,128)} %bitcast.6, f32[31,1024]{1,0:T(8,128)} %depth_in.1, f32[1,1024]{1,0:T(1,128)} %bitcast.7, bf16[1024,768]{1,0:T(8,128)(2,1)} %w_ref.1, ...), custom_call_target="tpu_custom_call" | custom-call | tf_op jit(solution)/shard_map/block/pallas_call | solution.py:544
  59.3 1.9 %copy.12 = bf16[1,256,1024]{2,1,0:T(8,128)(2,1)} copy(bf16[1,256,1024]{2,1,0:T(8,128)(2,1)} %block.1) | data formatting | bytes 1048576

commit v4 on v3

--- a/solution.py
+++ b/solution.py
@@ -51,10 +51,10 @@
 
 def block_kernel(
     blocks, groups, parts_of_chunk, head_width,
-    lengths_ref, frames_in, gain_in, conv_gain_in, depth_in, depth_gain_in,
+    lengths_in, frames_in, gain_in, conv_gain_in, depth_in, depth_gain_in,
     w_ref, w_out_ref, w_glu_ref, w_proj_ref,
     out_ref,
-    frames_ref, gain_ref, conv_gain_ref, depth_ref, depth_gain_ref, norm, held, weights, lent, q_ref, k_ref, v_ref, scores,
+    lengths_ref, frames_ref, gain_ref, conv_gain_ref, depth_ref, depth_gain_ref, norm, held, weights, lent, q_ref, k_ref, v_ref, scores,
     mixed_heads, parts, w_out, w_glu, w_proj, masks, residual, edge, halo, extended, mixed,
     load_sem, in_sem, ws_sem, wr_sem, d_sem, x_sem, y_sem, p_sem, r_sem, s_sem, a_sem, hs_sem, hr_sem,
 ):
@@ -79,8 +79,10 @@
     home = mine == g
     position = g * blocks + b
 
-    after = (position + 1) % (blocks * groups)
-    before = (position + blocks * groups - 1) % (blocks * groups)
+    last = blocks * groups - 1
+    after = jnp.minimum(position + 1, last)
+    before = jnp.maximum(position - 1, 0)
+    has_after, has_before = position < last, position > 0
     barrier = pltpu.get_barrier_semaphore()
 
     def hail(other_b, other_g):
@@ -115,7 +117,7 @@
     inputs = [
         pltpu.make_async_copy(src, dst, in_sem.at[i]) for i, (src, dst) in enumerate([
             (frames_in, frames_ref), (gain_in, gain_ref), (conv_gain_in, conv_gain_ref),
-            (depth_in, depth_ref), (depth_gain_in, depth_gain_ref),
+            (depth_in, depth_ref), (depth_gain_in, depth_gain_ref), (lengths_in, lengths_ref),
         ])
     ]
     for copy in inputs:
@@ -166,7 +168,7 @@
         )
 
     with jax.named_scope("in_wait"):
-        for copy in inputs:
+        for copy in inputs[:2]:
             copy.wait()
     with jax.named_scope("norm"):
         for c in range(chunks):
@@ -186,6 +188,8 @@
             def _():
                 held[b * chunks + c, at] = norm[c, at]
 
+    for copy in inputs[2:]:
+        copy.wait()
     load_lent.wait()
     for other in range(groups):
         source, copy = give(other)
@@ -225,10 +229,14 @@
             k_ref[h, at, :] = k.astype(jnp.bfloat16)
             v_ref[h, :head_width, at] = v.T.astype(jnp.bfloat16)
 
+    inner = step - side == reach - 1
+
     def unit(j, i, parity):
-        n = j // chunks
+        swap = jnp.logical_and(inner, step % 2 != parity)
+        n = jnp.where(swap, reach - 1 - j % reach, j // chunks)
+        c = jnp.where(swap, j // reach, j % chunks)
         n = n + side * (reach - 1 - 2 * n)
-        return ((2 * n + parity) * np_ + (share + i) % np_) * chunks + j % chunks
+        return ((2 * n + parity) * np_ + (share + i) % np_) * chunks + c
 
     def came(u, k):
         here = piece(held, u, k)
@@ -340,9 +348,14 @@
     tiles = blocks * block // tile
 
     def order(i):
-        n = i // np_
-        n = side * n + (1 - side) * (steps - 1 - n)
-        return n * np_ + (share + 1 + i) % np_
+        far = jnp.logical_or(i == 0, jnp.logical_and(i % 2 == 1, i < blocks - 1))
+        away = (i + 1) // 2
+        close = jnp.where(i == blocks - 1, blocks // 2 - 1, i // 2 - 1)
+        out_step = side * (away // np_) + (1 - side) * (steps - 1 - away // np_)
+        in_step = side * reach + (step - side * reach + 1 + close // np_) % reach
+        n = jnp.where(far, out_step, in_step)
+        m = jnp.where(far, away, close)
+        return n * np_ + (share + 1 + m) % np_
 
     def score(i, h, n, top):
         at = pl.ds(pl.multiple_of(order(i) * block, block), block)
@@ -442,8 +455,14 @@
     to_prev = remote(
         edge.at[0], halo.at[1], hs_sem.at[0], hr_sem.at[1], before % blocks, before // blocks
     )
-    to_next.start()
-    to_prev.start()
+
+    @pl.when(has_after)
+    def _():
+        to_next.start()
+
+    @pl.when(has_before)
+    def _():
+        to_prev.start()
 
     strip = min(64, block)
     spans = -(-taps // 8)
@@ -470,8 +489,17 @@
     with jax.named_scope("conv_mid"):
         convolve(every[1:-1])
     with jax.named_scope("halo_wait"):
-        to_next.wait_recv()
-        to_prev.wait_recv()
+        for i, present in ((0, has_before), (1, has_after)):
+            @pl.when(present)
+            def _():
+                remote(
+                    edge.at[i], halo.at[i], hs_sem.at[i], hr_sem.at[i], b, g
+                ).wait_recv()
+
+            @pl.when(jnp.logical_not(present))
+            def _():
+                halo[i] = jnp.zeros(halo.shape[1:], jnp.bfloat16)
+
     with jax.named_scope("conv_edge"):
         for c in range(width // 128):
             extended[c, :rim, :] = halo[0, :, 128 * c:128 * c + 128].astype(jnp.float32)
@@ -520,8 +548,13 @@
             def _():
                 send(i).wait_send()
 
-        to_next.wait_send()
-        to_prev.wait_send()
+        @pl.when(has_after)
+        def _():
+            to_next.wait_send()
+
+        @pl.when(has_before)
+        def _():
+            to_prev.wait_send()
 
 
 def body(
@@ -544,9 +577,10 @@
     return pl.pallas_call(
         functools.partial(block_kernel, blocks, groups, parts_of_chunk, head_width),
         out_shape=jax.ShapeDtypeStruct((1, rows, width), jnp.bfloat16),
-        in_specs=[pl.BlockSpec(memory_space=pltpu.SMEM)] + [hbm] * 9,
+        in_specs=[hbm] * 10,
         out_specs=vm,
         scratch_shapes=[
+            pltpu.SMEM(utt_lengths.shape, jnp.int32),
             pltpu.VMEM((rows, width), jnp.bfloat16),
             pltpu.VMEM((1, width), jnp.float32),
             pltpu.VMEM((1, width), jnp.float32),
@@ -572,7 +606,7 @@
             pltpu.VMEM((width // 128, rows + 2 * rim + 8, 128), jnp.float32),
             pltpu.VMEM((rows, width), jnp.float32),
             pltpu.SemaphoreType.DMA((5,)),
-            pltpu.SemaphoreType.DMA((5,)),
+            pltpu.SemaphoreType.DMA((6,)),
             pltpu.SemaphoreType.DMA((groups,)),
             pltpu.SemaphoreType.DMA((1,)),
             pltpu.SemaphoreType.DMA((chunks * parts_of_chunk,)),

time: 61.4 us -> 57.9 us (0.943)
  Pallas kernels: 59.3 us -> 55.8 us
    pallas_call x1, Pallas kernels: 59.3 us -> 55.8 us  [body(): pl.pallas_call(functools.partial(block_kernel, blocks, groups, parts_of_c...]
where the time goes in v4:
time: 57.9 us; the launch traced here: 57.7 us
  Pallas kernels  55.8 us (96%)
  local copies, waits for them, and re-layouts  1.87 us (3%)
    pallas_call x1, Pallas kernels, body(): pl.pallas_call(functools.partial(block_kernel, blocks, groups, parts_of_c...  55.8 us
    unnamed x1, local copies, waits for them, and re-layouts  1.87 us

profile of v4, /device:TPU:0, one launch (start us, length us, event | category | flops | bytes accessed | tf_op | source)
XLA Modules:
  0.0 57.7 jit_solution(13444987739457590238)
XLA Ops:
  0.0 55.8 %block.1 = bf16[1,256,1024]{2,1,0:T(8,128)(2,1)} custom-call(s32[4]{0:T(128)} %lengths_in.1, bf16[256,1024]{1,0:T(8,128)(2,1)} %bitcast.4, f32[1,1024]{1,0:T(1,128)} %bitcast.5, f32[1,1024]{1,0:T(1,128)} %bitcast.6, f32[31,1024]{1,0:T(8,128)} %depth_in.1, f32[1,1024]{1,0:T(1,128)} %bitcast.7, bf16[1024,768]{1,0:T(8,128)(2,1)} %w_ref.1, ...), custom_call_target="tpu_custom_call" | custom-call | tf_op jit(solution)/shard_map/block/pallas_call | solution.py:577
  55.8 1.9 %copy.12 = bf16[1,256,1024]{2,1,0:T(8,128)(2,1)} copy(bf16[1,256,1024]{2,1,0:T(8,128)(2,1)} %block.1) | data formatting | bytes 1048576

commit v5 on v4

--- a/solution.py
+++ b/solution.py
@@ -42,6 +42,15 @@
         src_ref=src, dst_ref=dst, send_sem=send, recv_sem=recv,
         device_id=(blk, grp), device_id_type=MESH,
     )
+
+
+def finished(mixed, residual, row_gain, w_proj):
+    normed = normalize(mixed, row_gain)
+    activated = (normed * jax.nn.sigmoid(normed)).astype(jnp.bfloat16)
+    return (
+        residual.astype(jnp.float32)
+        + jnp.dot(activated, w_proj, preferred_element_type=jnp.float32)
+    ).astype(jnp.bfloat16)
 
 
 def slot_of(b, g, blocks):
@@ -56,7 +65,7 @@
     out_ref,
     lengths_ref, frames_ref, gain_ref, conv_gain_ref, depth_ref, depth_gain_ref, norm, held, weights, lent, q_ref, k_ref, v_ref, scores,
     mixed_heads, parts, w_out, w_glu, w_proj, masks, residual, edge, halo, extended, mixed,
-    load_sem, in_sem, ws_sem, wr_sem, d_sem, x_sem, y_sem, p_sem, r_sem, s_sem, a_sem, hs_sem, hr_sem,
+    load_sem, in_sem, ws_sem, wr_sem, d_sem, x_sem, y_sem, z_sem, p_sem, r_sem, s_sem, a_sem, hs_sem, hr_sem,
 ):
     b, g = lax.axis_index("blk"), lax.axis_index("grp")
     np_ = blocks // groups
@@ -238,6 +247,31 @@
         n = n + side * (reach - 1 - 2 * n)
         return ((2 * n + parity) * np_ + (share + i) % np_) * chunks + c
 
+    lifts = reach == 2 and np_ > 1
+    inner_step, outer_step = reach - 1 + side, side * (steps - 1)
+
+    def lifted(u, at_inner):
+        return jnp.logical_and(at_inner, u // (chunks * np_) == outer_step)
+
+    def lift(j, i, k):
+        u = unit(j, i, core)
+        here = piece(held, u, k)
+        return remote(
+            here, here, z_sem.at[(j * (np_ - 1) + i - 1) * parts_of_chunk + k],
+            r_sem.at[u * parts_of_chunk + k],
+            (side * reach + (step - side * reach + 1) % reach) * np_ + share, g,
+        )
+
+    def crosses(j):
+        if lifts:
+            return jnp.logical_not(lifted(unit(j, 0, core), inner))
+        return j >= 0
+
+    def climbs(j, i):
+        return lifted(unit(j, i, core), jnp.logical_not(inner))
+
+    early = jnp.logical_and(step == outer_step, step % 2 == core)
+
     def came(u, k):
         here = piece(held, u, k)
         return remote(here, here, p_sem.at[0], r_sem.at[u * parts_of_chunk + k], b, partner)
@@ -254,7 +288,7 @@
         u = unit(j, 0, core)
         here = piece(held, u, k)
         return remote(
-            here, here, y_sem.at[(j * np_ + i - 1) * parts_of_chunk + k],
+            here, here, y_sem.at[(j * (np_ - 1) + i - 1) * parts_of_chunk + k],
             r_sem.at[u * parts_of_chunk + k], b - share + (share + i) % np_, g,
         )
 
@@ -284,8 +318,11 @@
                 for i in range(1, reach):
                     over(j, i, k).start()
 
-            for i in range(1, np_):
-                across(j, i, k).start()
+            @pl.when(crosses(j))
+            def _():
+                for i in range(1, np_):
+                    across(j, i, k).start()
+
             pair(j, 0, k).start()
 
     def arrive(u):
@@ -296,12 +333,22 @@
         for i in range(1, np_):
             for k in range(parts_of_chunk):
                 came(unit(j, i, core), k).wait_recv()
+                if lifts:
+                    @pl.when(climbs(j, i))
+                    def _():
+                        lift(j, i, k).start()
+
                 pair(j, i, k).start()
 
     with jax.named_scope("first"):
         take(0)
         take(1)
         pass_on(0)
+
+        @pl.when(early)
+        def _():
+            pass_on(1)
+
         if count > 2:
             take(2)
 
@@ -321,7 +368,7 @@
         def _():
             take(j + 3)
 
-        @pl.when(j >= 1)
+        @pl.when(jnp.logical_or(j >= 2, jnp.logical_and(j == 1, jnp.logical_not(early))))
         def _():
             pass_on(j)
 
@@ -422,18 +469,25 @@
         at = row + (t - half)
         masks[t] = jnp.where(jnp.logical_and(at >= low, at < high), 1.0, 0.0)
 
+    part_width = parts.shape[2]
+    together = max(1, 256 // part_width)
     with jax.named_scope("parts_wait"):
-        for i in range(blocks):
-            @pl.when(jnp.logical_not(jnp.logical_and(home, slot == i)))
-            def _():
-                remote(parts.at[i], parts.at[i], s_sem.at[i], a_sem.at[i], b, g).wait_recv()
+        loads[0].wait()
+        total = frames_ref[...].astype(jnp.float32)
+        for first in range(0, blocks, together):
+            for i in range(first, first + together):
+                @pl.when(jnp.logical_not(jnp.logical_and(home, slot == i)))
+                def _():
+                    remote(parts.at[i], parts.at[i], s_sem.at[i], a_sem.at[i], b, g).wait_recv()
+
+            attended = jnp.concatenate([parts[first + i] for i in range(together)], axis=1)
+            at = slice(first * part_width, (first + together) * part_width)
+            total = total + jnp.dot(attended, w_out[at, :], preferred_element_type=jnp.float32)
+            if first + together < blocks:
+                mixed[...] = total
+                total = mixed[...]
 
     with jax.named_scope("mid_mm"):
-        attended = jnp.concatenate([parts[i] for i in range(blocks)], axis=1)
-        loads[0].wait()
-        total = frames_ref[...].astype(jnp.float32) + jnp.dot(
-            attended, w_out[...], preferred_element_type=jnp.float32
-        )
         residual[...] = total.astype(jnp.bfloat16)
         conv_in = normalize(residual[...].astype(jnp.float32), conv_gain_ref[...]).astype(jnp.bfloat16)
         loads[1].wait()
@@ -464,30 +518,31 @@
     def _():
         to_prev.start()
 
-    strip = min(64, block)
     spans = -(-taps // 8)
 
     def convolve(strips):
         def column(c, carry):
             cols = pl.ds(pl.multiple_of(c * 128, 128), 128)
-            for r in strips:
+            for r, strip in strips:
                 acc = jnp.zeros((strip, 128), jnp.float32)
                 for p in range(8):
                     o = rim + r + p - half
                     slab = extended[c, o:o + strip + 8 * (spans - 1), :]
-                    for j in range(spans):
-                        t = 8 * j + p
-                        if t < taps:
-                            x = slab[8 * j:8 * j + strip] * masks[t, r:r + strip, :]
-                            acc = acc + x * depth_ref[t:t + 1, cols]
+                    for t in range(p, taps, 8):
+                        x = slab[t - p:t - p + strip] * masks[t, r:r + strip, :]
+                        acc = acc + x * depth_ref[t:t + 1, cols]
                 mixed[r:r + strip, cols] = acc
             return carry
 
         lax.fori_loop(0, width // 128, column, 0)
 
-    every = list(range(0, block, strip))
     with jax.named_scope("conv_mid"):
-        convolve(every[1:-1])
+        convolve([(r, min(64, block - rim - r)) for r in range(rim, block - rim, 64)])
+    with jax.named_scope("tail_mm"):
+        loads[2].wait()
+        out_ref[0, rim:block - rim] = finished(
+            mixed[rim:block - rim], residual[rim:block - rim], depth_gain_ref[...], w_proj[...]
+        )
     with jax.named_scope("halo_wait"):
         for i, present in ((0, has_before), (1, has_after)):
             @pl.when(present)
@@ -502,17 +557,18 @@
 
     with jax.named_scope("conv_edge"):
         for c in range(width // 128):
-            extended[c, :rim, :] = halo[0, :, 128 * c:128 * c + 128].astype(jnp.float32)
-            extended[c, rim + block:2 * rim + block, :] = halo[1, :, 128 * c:128 * c + 128].astype(jnp.float32)
-        convolve([every[0], every[-1]])
-    with jax.named_scope("tail_mm"):
-        normed = normalize(mixed[...], depth_gain_ref[...])
-        activated = (normed * jax.nn.sigmoid(normed)).astype(jnp.bfloat16)
-        loads[2].wait()
-        out_ref[0] = (
-            residual[...].astype(jnp.float32)
-            + jnp.dot(activated, w_proj[...], preferred_element_type=jnp.float32)
-        ).astype(out_ref.dtype)
+            at = slice(128 * c, 128 * c + 128)
+            extended[c, :rim, :] = halo[0, :, at].astype(jnp.float32)
+            extended[c, rim + block:2 * rim + block, :] = halo[1, :, at].astype(jnp.float32)
+        convolve([(0, rim), (block - rim, rim)])
+    with jax.named_scope("tail_edge"):
+        ends = finished(
+            jnp.concatenate([mixed[:rim], mixed[block - rim:]], axis=0),
+            jnp.concatenate([residual[:rim], residual[block - rim:]], axis=0),
+            depth_gain_ref[...], w_proj[...],
+        )
+        out_ref[0, :rim] = ends[:rim]
+        out_ref[0, block - rim:] = ends[rim:]
 
     with jax.named_scope("drain"):
         for c in range(chunks):
@@ -535,8 +591,17 @@
                     for i in range(1, reach):
                         over(j, i, k).wait_send()
 
-                for i in range(1, np_):
-                    across(j, i, k).wait_send()
+                @pl.when(crosses(j))
+                def _():
+                    for i in range(1, np_):
+                        across(j, i, k).wait_send()
+
+                if lifts:
+                    for i in range(1, np_):
+                        @pl.when(climbs(j, i))
+                        def _():
+                            lift(j, i, k).wait_send()
+
                 for i in range(np_):
                     pair(j, i, k).wait_send()
             return carry
@@ -611,7 +676,8 @@
             pltpu.SemaphoreType.DMA((1,)),
             pltpu.SemaphoreType.DMA((chunks * parts_of_chunk,)),
             pltpu.SemaphoreType.DMA((reach * chunks * (reach - 1) * parts_of_chunk,)),
-            pltpu.SemaphoreType.DMA((reach * chunks * np_ * parts_of_chunk,)),
+            pltpu.SemaphoreType.DMA((reach * chunks * max(np_ - 1, 1) * parts_of_chunk,)),
+            pltpu.SemaphoreType.DMA((reach * chunks * max(np_ - 1, 1) * parts_of_chunk,)),
             pltpu.SemaphoreType.DMA((reach * chunks * np_ * parts_of_chunk,)),
             pltpu.SemaphoreType.DMA((blocks * chunks * parts_of_chunk,)),
             pltpu.SemaphoreType.DMA((blocks,)),

time: 57.9 us -> 57.3 us (0.990)
  Pallas kernels: 55.8 us -> 55.2 us
where the time goes in v5:
time: 57.3 us; the launch traced here: 57.1 us
  Pallas kernels  55.2 us (96%)
  local copies, waits for them, and re-layouts  1.87 us (3%)
    pallas_call x1, Pallas kernels, body(): pl.pallas_call(functools.partial(block_kernel, blocks, groups, parts_of_c...  55.2 us
    unnamed x1, local copies, waits for them, and re-layouts  1.87 us

profile of v5, /device:TPU:0, one launch (start us, length us, event | category | flops | bytes accessed | tf_op | source)
XLA Modules:
  0.0 57.1 jit_solution(5623650567035399794)
XLA Ops:
  0.0 55.2 %block.1 = bf16[1,256,1024]{2,1,0:T(8,128)(2,1)} custom-call(s32[4]{0:T(128)} %lengths_in.1, bf16[256,1024]{1,0:T(8,128)(2,1)} %bitcast.4, f32[1,1024]{1,0:T(1,128)} %bitcast.5, f32[1,1024]{1,0:T(1,128)} %bitcast.6, f32[31,1024]{1,0:T(8,128)} %depth_in.1, f32[1,1024]{1,0:T(1,128)} %bitcast.7, bf16[1024,768]{1,0:T(8,128)(2,1)} %w_ref.1, ...), custom_call_target="tpu_custom_call" | custom-call | tf_op jit(solution)/shard_map/block/pallas_call | solution.py:642
  55.3 1.9 %copy.12 = bf16[1,256,1024]{2,1,0:T(8,128)(2,1)} copy(bf16[1,256,1024]{2,1,0:T(8,128)(2,1)} %block.1) | data formatting | bytes 1048576

commit v6 on v5

--- a/solution.py
+++ b/solution.py
@@ -391,7 +391,7 @@
             mixed_heads.at[s], parts.at[slot], s_sem.at[s], a_sem.at[slot], s, mine
         )
 
-    tile = min(512, blocks * block)
+    tile = min(1024, blocks * block)
     tiles = blocks * block // tile
 
     def order(i):

time: 57.3 us -> 57.1 us (level)
  no operation moved by 1% of the time
where the time goes in v6:
time: 57.1 us; the launch traced here: 56.9 us
  Pallas kernels  55 us (96%)
  local copies, waits for them, and re-layouts  1.87 us (3%)
    pallas_call x1, Pallas kernels, body(): pl.pallas_call(functools.partial(block_kernel, blocks, groups, parts_of_c...  55 us
    unnamed x1, local copies, waits for them, and re-layouts  1.87 us

profile of v6, /device:TPU:0, one launch (start us, length us, event | category | flops | bytes accessed | tf_op | source)
XLA Modules:
  0.0 56.9 jit_solution(6322259508757171369)
XLA Ops:
  0.0 55.0 %block.1 = bf16[1,256,1024]{2,1,0:T(8,128)(2,1)} custom-call(s32[4]{0:T(128)} %lengths_in.1, bf16[256,1024]{1,0:T(8,128)(2,1)} %bitcast.4, f32[1,1024]{1,0:T(1,128)} %bitcast.5, f32[1,1024]{1,0:T(1,128)} %bitcast.6, f32[31,1024]{1,0:T(8,128)} %depth_in.1, f32[1,1024]{1,0:T(1,128)} %bitcast.7, bf16[1024,768]{1,0:T(8,128)(2,1)} %w_ref.1, ...), custom_call_target="tpu_custom_call" | custom-call | tf_op jit(solution)/shard_map/block/pallas_call | solution.py:642
  55.1 1.9 %copy.12 = bf16[1,256,1024]{2,1,0:T(8,128)(2,1)} copy(bf16[1,256,1024]{2,1,0:T(8,128)(2,1)} %block.1) | data formatting | bytes 1048576
